TPU v7x, 32 devices: a whole 2x2x4 slice. The times are simulated.
32 devices in a mesh: gx: 4 (over z), gy: 4 (over x, core), gz: 2 (over y).
Axes of the slice: x: 2, y: 2, z: 4, core: 2. Of those that a mesh axis runs over, the one named last changes fastest.
Arguments:
- populations: float32 [19, 16, 32, 512], P(None, 'gz', 'gx', 'gy'), may hold values from 0 to 1, as said below
- omega: float32 [16, 32, 512], P('gz', 'gx', 'gy'), may hold values from 0.8 to 1.7
- obstacle: int32 [16, 32, 512], P('gz', 'gx', 'gy'), may hold values 0 or 1
Outputs:
- lifted: float32 [19, 16, 32, 512], P(None, 'gz', 'gx', 'gy')
- diagnostics: float32 [5], replicated
Inputs may be any that keep to these rules, and one draw needn't show every extreme that they name: `populations`: every population lies between 0.3 and 1.7 times its lattice weight.
All inputs are finite; a program needn't handle non-finite values. No bound on the sum of `obstacle` on one device may be relied on, other than what follows from the above.
Results may differ from a plain program's by a relative error of at most 0.0001.
Values sent between devices are 32-bit elements; how exact they have to be, the bound alone decides.
A program may use at most 128 MiB of HBM per device.

v0:
```python
import jax
import jax.numpy as jnp
from jax import lax
from jax.sharding import PartitionSpec as P

STEPS = 4
JUMP = 2
lattice = [
    (0, 0, 0),
    (1, 0, 0),
    (-1, 0, 0),
    (0, 1, 0),
    (0, -1, 0),
    (0, 0, 1),
    (0, 0, -1),
    (1, 1, 0),
    (-1, -1, 0),
    (1, -1, 0),
    (-1, 1, 0),
    (1, 0, 1),
    (-1, 0, -1),
    (1, 0, -1),
    (-1, 0, 1),
    (0, 1, 1),
    (0, -1, -1),
    (0, 1, -1),
    (0, -1, 1),
]
weights = [1.0 / 3.0] + [1.0 / 18.0] * 6 + [1.0 / 36.0] * 12
opposite = [0, 2, 1, 4, 3, 6, 5, 8, 7, 10, 9, 12, 11, 14, 13, 16, 15, 18, 17]
limiter = 25.0


def extended(x, sides, width):
    for axis, dim in sides:
        size, length = (lax.axis_size(axis), x.shape[dim])
        up = [(i, (i + 1) % size) for i in range(size)]
        down = [(j, i) for i, j in up]
        last = lax.slice_in_dim(x, length - width, length, axis=dim)
        first = lax.slice_in_dim(x, 0, width, axis=dim)
        before = lax.ppermute(last, axis, up)
        after = lax.ppermute(first, axis, down)
        x = jnp.concatenate([before, x, after], axis=dim)
    return x


def moments(f):
    rho = jnp.sum(f, axis=0)
    comps = []
    for axis_pick in range(3):
        total = jnp.zeros_like(rho)
        for index in range(19):
            comp = lattice[index][axis_pick]
            if comp != 0:
                total = total + comp * f[index]
        comps.append(total)
    return (rho, comps[0], comps[1], comps[2])


def equilibrium(rho, momx, momy, momz):
    safe = jnp.maximum(rho, 0.5)
    velx, vely, velz = (momx / safe, momy / safe, momz / safe)
    square = velx * velx + vely * vely + velz * velz
    rows = []
    for index in range(19):
        cx, cy, cz = lattice[index]
        proj = cx * velx + cy * vely + cz * velz
        rows.append(weights[index] * rho * (1.0 + 3.0 * proj + 4.5 * proj * proj - 1.5 * square))
    return jnp.stack(rows, 0)


def collide(f, omega, solid):
    rho, momx, momy, momz = moments(f)
    feq = equilibrium(rho, momx, momy, momz)
    post = f + omega[None] * (feq - f)
    flipped = jnp.stack([f[opposite[index]] for index in range(19)], 0)
    return jnp.where(solid[None], flipped, post)


def stream(padded):
    size_z = padded.shape[1] - 2
    size_x = padded.shape[2] - 2
    size_y = padded.shape[3] - 2
    rows = []
    for index in range(19):
        cx, cy, cz = lattice[index]
        rows.append(
            padded[
                index, 1 - cz : 1 - cz + size_z, 1 - cx : 1 - cx + size_x, 1 - cy : 1 - cy + size_y
            ]
        )
    return jnp.stack(rows, 0)


def per_device(populations, omega, obstacle):
    solid = obstacle == 1
    f = populations
    before = f
    for step in range(STEPS):
        post = collide(f, omega, solid)
        padded = extended(post, (("gx", 2), ("gy", 3), ("gz", 1)), 1)
        f = stream(padded)
        if step == STEPS - 2:
            before = f
    rho_a, jxa, jya, jza = moments(before)
    rho_b, jxb, jyb, jzb = moments(f)
    cells = float(
        f.shape[1]
        * f.shape[2]
        * f.shape[3]
        * lax.axis_size("gx")
        * lax.axis_size("gy")
        * lax.axis_size("gz")
    )
    diff_rho = rho_b - rho_a
    diff_x = jxb - jxa
    diff_y = jyb - jya
    diff_z = jzb - jza
    local_terms = (
        jnp.sum(diff_rho * diff_rho),
        jnp.sum(diff_x * diff_x + diff_y * diff_y + diff_z * diff_z),
        jnp.sum(jxb),
        jnp.sum(jyb),
        jnp.sum(jzb),
        jnp.sum(diff_x),
        jnp.sum(diff_y),
        jnp.sum(diff_z),
        jnp.sum(jxb * jxb + jyb * jyb + jzb * jzb),
        jnp.sum(jxb * diff_x + jyb * diff_y + jzb * diff_z),
    )
    (
        change_rho,
        change_mom,
        base_x,
        base_y,
        base_z,
        delta_x,
        delta_y,
        delta_z,
        energy_base,
        energy_cross,
    ) = lax.psum(
        (
            local_terms[0],
            local_terms[1],
            local_terms[2],
            local_terms[3],
            local_terms[4],
            local_terms[5],
            local_terms[6],
            local_terms[7],
            local_terms[8],
            local_terms[9],
        ),
        ("gx", "gy", "gz"),
    )
    change = (change_rho + change_mom) / cells
    gain = JUMP / (1.0 + limiter * change)
    jxp = jxb + gain * diff_x
    jyp = jyb + gain * diff_y
    jzp = jzb + gain * diff_z
    sum_x = base_x + gain * delta_x
    sum_y = base_y + gain * delta_y
    sum_z = base_z + gain * delta_z
    energy = energy_base + 2.0 * gain * energy_cross + gain * gain * change_mom
    rho_p = rho_b + gain * diff_rho
    lifted = equilibrium(rho_p, jxp, jyp, jzp)
    diagnostics = jnp.stack([change, sum_x / cells, sum_y / cells, sum_z / cells, energy / cells])
    return (lifted, diagnostics)


def solution(mesh):
    in_specs = (P(None, "gz", "gx", "gy"), P("gz", "gx", "gy"), P("gz", "gx", "gy"))
    out_specs = (P(None, "gz", "gx", "gy"), P())
    return jax.shard_map(
        per_device, mesh=mesh, in_specs=in_specs, out_specs=out_specs, check_vma=False
    )
```

profile of v0, /device:TPU:12, one launch (start us, length us, event | category | flops | bytes accessed | tf_op | source)
XLA Modules:
  0.0 191.7 jit_solution(2588128891063399128)
XLA Ops:
  5.9 1.6 collective-permute-start.1
  7.5 2.4 %collective-permute-done = f32[19,8,1,128]{3,2,1,0:T(1,128)S(1)} collective-permute-done((f32[19,8,1,128]{3,2,1,0:T(1,128)S(1)}, f32[19,8,1,128]{3,2,1,0:T(1,128)S(1)}, u32[]{:S(2)}, u32[]{:S(2)}) %collective-permute-start) | collective-permute-done | bytes 77856 | tf_op jit(solution)/shard_map/ppermute | solution.py:42
  9.8 3.4 %collective-permute-done.1 = f32[19,8,1,128]{3,2,1,0:T(1,128)S(1)} collective-permute-done((f32[19,8,1,128]{3,2,1,0:T(1,128)S(1)}, f32[19,8,1,128]{3,2,1,0:T(1,128)S(1)}, u32[]{:S(2)}, u32[]{:S(2)}) %collective-permute-start.1) | collective-permute-done | bytes 77856 | tf_op jit(solution)/shard_map/ppermute | solution.py:41
  21.2 1.5 collective-permute-start.5
  22.8 8.1 %collective-permute-done.4 = f32[19,1,10,130]{3,2,1,0:T(8,128)S(1)} collective-permute-done((f32[19,1,10,130]{3,2,1,0:T(8,128)S(1)}, f32[19,1,10,130]{3,2,1,0:T(8,128)S(1)}, u32[]{:S(2)}, u32[]{:S(2)}) %collective-permute-start.4) | collective-permute-done | bytes 98832 | tf_op jit(solution)/shard_map/ppermute | solution.py:42
  31.0 6.2 %collective-permute-done.5 = f32[19,1,10,130]{3,2,1,0:T(8,128)S(1)} collective-permute-done((f32[19,1,10,130]{3,2,1,0:T(8,128)S(1)}, f32[19,1,10,130]{3,2,1,0:T(8,128)S(1)}, u32[]{:S(2)}, u32[]{:S(2)}) %collective-permute-start.5) | collective-permute-done | bytes 98832 | tf_op jit(solution)/shard_map/ppermute | solution.py:41
  38.8 2.5 %collective-permute-start.6 = (f32[19,8,1,128]{3,2,1,0:T(1,128)S(1)}, f32[19,8,1,128]{3,2,1,0:T(1,128)S(1)}, u32[]{:S(2)}, u32[]{:S(2)}) collective-permute-start(f32[19,8,1,128]{3,2,1,0:T(1,128)S(1)} %get-tuple-element.150), channel_id=1, source_target_pairs={{8,0},{16,8},{24,16},{0,24},{9,1},{17,9},{25,17},{1,25},{10,2},{18... | collective-permute-start | bytes 233480 | tf_op jit(solution)/shard_map/ppermute | solution.py:42
  41.3 2.0 %collective-permute-done.6 = f32[19,8,1,128]{3,2,1,0:T(1,128)S(1)} collective-permute-done((f32[19,8,1,128]{3,2,1,0:T(1,128)S(1)}, f32[19,8,1,128]{3,2,1,0:T(1,128)S(1)}, u32[]{:S(2)}, u32[]{:S(2)}) %collective-permute-start.6) | collective-permute-done | bytes 77856 | tf_op jit(solution)/shard_map/ppermute | solution.py:42
  43.3 2.4 %collective-permute-done.7 = f32[19,8,1,128]{3,2,1,0:T(1,128)S(1)} collective-permute-done((f32[19,8,1,128]{3,2,1,0:T(1,128)S(1)}, f32[19,8,1,128]{3,2,1,0:T(1,128)S(1)}, u32[]{:S(2)}, u32[]{:S(2)}) %collective-permute-start.7) | collective-permute-done | bytes 77856 | tf_op jit(solution)/shard_map/ppermute | solution.py:41
  53.9 1.5 collective-permute-start.11
  55.5 8.1 %collective-permute-done.10 = f32[19,1,10,130]{3,2,1,0:T(8,128)S(1)} collective-permute-done((f32[19,1,10,130]{3,2,1,0:T(8,128)S(1)}, f32[19,1,10,130]{3,2,1,0:T(8,128)S(1)}, u32[]{:S(2)}, u32[]{:S(2)}) %collective-permute-start.10) | collective-permute-done | bytes 98832 | tf_op jit(solution)/shard_map/ppermute | solution.py:42
  63.6 5.0 %collective-permute-done.11 = f32[19,1,10,130]{3,2,1,0:T(8,128)S(1)} collective-permute-done((f32[19,1,10,130]{3,2,1,0:T(8,128)S(1)}, f32[19,1,10,130]{3,2,1,0:T(8,128)S(1)}, u32[]{:S(2)}, u32[]{:S(2)}) %collective-permute-start.11) | collective-permute-done | bytes 98832 | tf_op jit(solution)/shard_map/ppermute | solution.py:41
  70.3 2.4 %collective-permute-start.12 = (f32[19,8,1,128]{3,2,1,0:T(1,128)S(1)}, f32[19,8,1,128]{3,2,1,0:T(1,128)S(1)}, u32[]{:S(2)}, u32[]{:S(2)}) collective-permute-start(f32[19,8,1,128]{3,2,1,0:T(1,128)S(1)} %get-tuple-element.148), channel_id=1, source_target_pairs={{8,0},{16,8},{24,16},{0,24},{9,1},{17,9},{25,17},{1,25},{10,2},{18... | collective-permute-start | bytes 233480 | tf_op jit(solution)/shard_map/ppermute | solution.py:42
  72.6 2.9 %collective-permute-done.12 = f32[19,8,1,128]{3,2,1,0:T(1,128)S(1)} collective-permute-done((f32[19,8,1,128]{3,2,1,0:T(1,128)S(1)}, f32[19,8,1,128]{3,2,1,0:T(1,128)S(1)}, u32[]{:S(2)}, u32[]{:S(2)}) %collective-permute-start.12) | collective-permute-done | bytes 77856 | tf_op jit(solution)/shard_map/ppermute | solution.py:42
  86.7 8.1 %collective-permute-done.16 = f32[19,1,10,130]{3,2,1,0:T(8,128)S(1)} collective-permute-done((f32[19,1,10,130]{3,2,1,0:T(8,128)S(1)}, f32[19,1,10,130]{3,2,1,0:T(8,128)S(1)}, u32[]{:S(2)}, u32[]{:S(2)}) %collective-permute-start.16) | collective-permute-done | bytes 98832 | tf_op jit(solution)/shard_map/ppermute | solution.py:42
  94.8 6.2 %collective-permute-done.17 = f32[19,1,10,130]{3,2,1,0:T(8,128)S(1)} collective-permute-done((f32[19,1,10,130]{3,2,1,0:T(8,128)S(1)}, f32[19,1,10,130]{3,2,1,0:T(8,128)S(1)}, u32[]{:S(2)}, u32[]{:S(2)}) %collective-permute-start.17) | collective-permute-done | bytes 98832 | tf_op jit(solution)/shard_map/ppermute | solution.py:41
  104.3 1.6 collective-permute-start.19
  105.9 2.3 %collective-permute-done.18 = f32[19,8,1,128]{3,2,1,0:T(1,128)S(1)} collective-permute-done((f32[19,8,1,128]{3,2,1,0:T(1,128)S(1)}, f32[19,8,1,128]{3,2,1,0:T(1,128)S(1)}, u32[]{:S(2)}, u32[]{:S(2)}) %collective-permute-start.18) | collective-permute-done | bytes 77856 | tf_op jit(solution)/shard_map/ppermute | solution.py:41
  112.2 1.8 collective-permute-start.21
  116.6 2.2 %copy.221 = f32[19,8,10,1]{3,2,1,0:T(8,128)S(1)} copy(f32[19,8,10,1]{0,1,3,2:T(8,128)} %collective-permute-done.21) | data formatting | bytes 12160 | tf_op jit(solution)/shard_map/ppermute | solution.py:42
  119.9 1.6 collective-permute-start.23
  121.5 8.1 %collective-permute-done.22 = f32[19,1,10,130]{3,2,1,0:T(8,128)S(1)} collective-permute-done((f32[19,1,10,130]{3,2,1,0:T(8,128)S(1)}, f32[19,1,10,130]{3,2,1,0:T(8,128)S(1)}, u32[]{:S(2)}, u32[]{:S(2)}) %collective-permute-start.22) | collective-permute-done | bytes 98832 | tf_op jit(solution)/shard_map/ppermute | solution.py:41
  129.6 4.6 %collective-permute-done.23 = f32[19,1,10,130]{3,2,1,0:T(8,128)S(1)} collective-permute-done((f32[19,1,10,130]{3,2,1,0:T(8,128)S(1)}, f32[19,1,10,130]{3,2,1,0:T(8,128)S(1)}, u32[]{:S(2)}, u32[]{:S(2)}) %collective-permute-start.23) | collective-permute-done | bytes 98832 | tf_op jit(solution)/shard_map/ppermute | solution.py:42
  137.9 44.2 %all-reduce = (f32[]{:T(128)}, f32[]{:T(128)}, f32[]{:T(128)}, f32[]{:T(128)}, f32[]{:T(128)}, /*index=5*/f32[]{:T(128)}, f32[]{:T(128)}, f32[]{:T(128)}, f32[]{:T(128)}, f32[]{:T(128)}) all-reduce(f32[]{:T(128)} %fusion.287, f32[]{:T(128)} %get-tuple-element.5, ...), channel_id=1, replica_groups=mesh['gx'=4,'gy'=4,'gz'=2] {'gx','gy','gz'}, use_global_device_ids=true, to_apply=%region_2.3 | all-reduce | flops 10 | bytes 80 | tf_op jit(solution)/shard_map/psum | solution.py:142
  (381 shorter events, 50.8 us)
Async XLA Ops:
  5.4 4.5 %collective-permute-start = (f32[19,8,1,128]{3,2,1,0:T(1,128)S(1)}, f32[19,8,1,128]{3,2,1,0:T(1,128)S(1)}, u32[]{:S(2)}, u32[]{:S(2)}) collective-permute-start(f32[19,8,1,128]{3,2,1,0:T(1,128)S(1)} %get-tuple-element.152), channel_id=1, source_target_pairs={{8,0},{16,8},{24,16},{0,24},{9,1},{17,9},{25,17},{1,25},{10,2},{18... | collective-permute-start | bytes 233480 | tf_op jit(solution)/shard_map/ppermute | solution.py:42
  5.9 7.3 %collective-permute-start.1 = (f32[19,8,1,128]{3,2,1,0:T(1,128)S(1)}, f32[19,8,1,128]{3,2,1,0:T(1,128)S(1)}, u32[]{:S(2)}, u32[]{:S(2)}) collective-permute-start(f32[19,8,1,128]{3,2,1,0:T(1,128)S(1)} %get-tuple-element.151), channel_id=1, source_target_pairs={{0,8},{8,16},{16,24},{24,0},{1,9},{9,17},{17,25},{25,1},{2,10},{10... | collective-permute-start | bytes 233480 | tf_op jit(solution)/shard_map/ppermute | solution.py:41
  14.6 1.7 collective-permute-start.2
  15.4 3.5 %collective-permute-start.3 = (f32[19,8,10,1]{0,1,3,2:T(8,128)S(1)}, f32[19,8,10,1]{0,1,3,2:T(8,128)S(1)}, u32[]{:S(2)}, u32[]{:S(2)}) collective-permute-start(f32[19,8,10,1]{0,1,3,2:T(8,128)S(1)} %copy.202), channel_id=1, source_target_pairs={{0,2},{2,4},{4,6},{6,0},{1,3},{3,5},{5,7},{7,1},{8,10},{10,12},{12... | collective-permute-start | bytes 18248 | tf_op jit(solution)/shard_map/ppermute | solution.py:41
  20.7 10.3 %collective-permute-start.4 = (f32[19,1,10,130]{3,2,1,0:T(8,128)S(1)}, f32[19,1,10,130]{3,2,1,0:T(8,128)S(1)}, u32[]{:S(2)}, u32[]{:S(2)}) collective-permute-start(f32[19,1,10,130]{3,2,1,0:T(8,128)S(1)} %get-tuple-element.136), channel_id=1, source_target_pairs={{1,0},{0,1},{3,2},{2,3},{5,4},{4,5},{7,6},{6,7},{9,8},{8,9},{11,10... | collective-permute-start | bytes 296408 | tf_op jit(solution)/shard_map/ppermute | solution.py:42
  21.2 15.9 %collective-permute-start.5 = (f32[19,1,10,130]{3,2,1,0:T(8,128)S(1)}, f32[19,1,10,130]{3,2,1,0:T(8,128)S(1)}, u32[]{:S(2)}, u32[]{:S(2)}) collective-permute-start(f32[19,1,10,130]{3,2,1,0:T(8,128)S(1)} %get-tuple-element.135), channel_id=1, source_target_pairs={{0,1},{1,0},{2,3},{3,2},{4,5},{5,4},{6,7},{7,6},{8,9},{9,8},{10,11... | collective-permute-start | bytes 296408 | tf_op jit(solution)/shard_map/ppermute | solution.py:41
  38.8 4.5 %collective-permute-start.6 = (f32[19,8,1,128]{3,2,1,0:T(1,128)S(1)}, f32[19,8,1,128]{3,2,1,0:T(1,128)S(1)}, u32[]{:S(2)}, u32[]{:S(2)}) collective-permute-start(f32[19,8,1,128]{3,2,1,0:T(1,128)S(1)} %get-tuple-element.150), channel_id=1, source_target_pairs={{8,0},{16,8},{24,16},{0,24},{9,1},{17,9},{25,17},{1,25},{10,2},{18... | collective-permute-start | bytes 233480 | tf_op jit(solution)/shard_map/ppermute | solution.py:42
  41.3 4.5 %collective-permute-start.7 = (f32[19,8,1,128]{3,2,1,0:T(1,128)S(1)}, f32[19,8,1,128]{3,2,1,0:T(1,128)S(1)}, u32[]{:S(2)}, u32[]{:S(2)}) collective-permute-start(f32[19,8,1,128]{3,2,1,0:T(1,128)S(1)} %get-tuple-element.149), channel_id=1, source_target_pairs={{0,8},{8,16},{16,24},{24,0},{1,9},{9,17},{17,25},{25,1},{2,10},{10... | collective-permute-start | bytes 233480 | tf_op jit(solution)/shard_map/ppermute | solution.py:41
  47.1 1.7 collective-permute-start.8
  47.9 3.6 %collective-permute-start.9 = (f32[19,8,10,1]{0,1,3,2:T(8,128)S(1)}, f32[19,8,10,1]{0,1,3,2:T(8,128)S(1)}, u32[]{:S(2)}, u32[]{:S(2)}) collective-permute-start(f32[19,8,10,1]{0,1,3,2:T(8,128)S(1)} %copy.208), channel_id=1, source_target_pairs={{0,2},{2,4},{4,6},{6,0},{1,3},{3,5},{5,7},{7,1},{8,10},{10,12},{12... | collective-permute-start | bytes 18248 | tf_op jit(solution)/shard_map/ppermute | solution.py:41
  53.3 10.3 %collective-permute-start.10 = (f32[19,1,10,130]{3,2,1,0:T(8,128)S(1)}, f32[19,1,10,130]{3,2,1,0:T(8,128)S(1)}, u32[]{:S(2)}, u32[]{:S(2)}) collective-permute-start(f32[19,1,10,130]{3,2,1,0:T(8,128)S(1)} %get-tuple-element.134), channel_id=1, source_target_pairs={{1,0},{0,1},{3,2},{2,3},{5,4},{4,5},{7,6},{6,7},{9,8},{8,9},{11,10... | collective-permute-start | bytes 296408 | tf_op jit(solution)/shard_map/ppermute | solution.py:42
  53.9 14.8 %collective-permute-start.11 = (f32[19,1,10,130]{3,2,1,0:T(8,128)S(1)}, f32[19,1,10,130]{3,2,1,0:T(8,128)S(1)}, u32[]{:S(2)}, u32[]{:S(2)}) collective-permute-start(f32[19,1,10,130]{3,2,1,0:T(8,128)S(1)} %get-tuple-element.133), channel_id=1, source_target_pairs={{0,1},{1,0},{2,3},{3,2},{4,5},{5,4},{6,7},{7,6},{8,9},{9,8},{10,11... | collective-permute-start | bytes 296408 | tf_op jit(solution)/shard_map/ppermute | solution.py:41
  70.3 5.3 %collective-permute-start.12 = (f32[19,8,1,128]{3,2,1,0:T(1,128)S(1)}, f32[19,8,1,128]{3,2,1,0:T(1,128)S(1)}, u32[]{:S(2)}, u32[]{:S(2)}) collective-permute-start(f32[19,8,1,128]{3,2,1,0:T(1,128)S(1)} %get-tuple-element.148), channel_id=1, source_target_pairs={{8,0},{16,8},{24,16},{0,24},{9,1},{17,9},{25,17},{1,25},{10,2},{18... | collective-permute-start | bytes 233480 | tf_op jit(solution)/shard_map/ppermute | solution.py:42
  72.6 4.4 %collective-permute-start.13 = (f32[19,8,1,128]{3,2,1,0:T(1,128)S(1)}, f32[19,8,1,128]{3,2,1,0:T(1,128)S(1)}, u32[]{:S(2)}, u32[]{:S(2)}) collective-permute-start(f32[19,8,1,128]{3,2,1,0:T(1,128)S(1)} %get-tuple-element.147), channel_id=1, source_target_pairs={{0,8},{8,16},{16,24},{24,0},{1,9},{9,17},{17,25},{25,1},{2,10},{10... | collective-permute-start | bytes 233480 | tf_op jit(solution)/shard_map/ppermute | solution.py:41
  78.4 1.7 collective-permute-start.14
  79.2 3.5 %collective-permute-start.15 = (f32[19,8,10,1]{0,1,3,2:T(8,128)S(1)}, f32[19,8,10,1]{0,1,3,2:T(8,128)S(1)}, u32[]{:S(2)}, u32[]{:S(2)}) collective-permute-start(f32[19,8,10,1]{0,1,3,2:T(8,128)S(1)} %copy.214), channel_id=1, source_target_pairs={{0,2},{2,4},{4,6},{6,0},{1,3},{3,5},{5,7},{7,1},{8,10},{10,12},{12... | collective-permute-start | bytes 18248 | tf_op jit(solution)/shard_map/ppermute | solution.py:41
  84.5 10.3 %collective-permute-start.16 = (f32[19,1,10,130]{3,2,1,0:T(8,128)S(1)}, f32[19,1,10,130]{3,2,1,0:T(8,128)S(1)}, u32[]{:S(2)}, u32[]{:S(2)}) collective-permute-start(f32[19,1,10,130]{3,2,1,0:T(8,128)S(1)} %get-tuple-element.132), channel_id=1, source_target_pairs={{1,0},{0,1},{3,2},{2,3},{5,4},{4,5},{7,6},{6,7},{9,8},{8,9},{11,10... | collective-permute-start | bytes 296408 | tf_op jit(solution)/shard_map/ppermute | solution.py:42
  85.1 15.9 %collective-permute-start.17 = (f32[19,1,10,130]{3,2,1,0:T(8,128)S(1)}, f32[19,1,10,130]{3,2,1,0:T(8,128)S(1)}, u32[]{:S(2)}, u32[]{:S(2)}) collective-permute-start(f32[19,1,10,130]{3,2,1,0:T(8,128)S(1)} %get-tuple-element.131), channel_id=1, source_target_pairs={{0,1},{1,0},{2,3},{3,2},{4,5},{5,4},{6,7},{7,6},{8,9},{9,8},{10,11... | collective-permute-start | bytes 296408 | tf_op jit(solution)/shard_map/ppermute | solution.py:41
  103.3 5.0 %collective-permute-start.18 = (f32[19,8,1,128]{3,2,1,0:T(1,128)S(1)}, f32[19,8,1,128]{3,2,1,0:T(1,128)S(1)}, u32[]{:S(2)}, u32[]{:S(2)}) collective-permute-start(f32[19,8,1,128]{3,2,1,0:T(1,128)S(1)} %get-tuple-element.146), channel_id=1, source_target_pairs={{0,8},{8,16},{16,24},{24,0},{1,9},{9,17},{17,25},{25,1},{2,10},{10... | collective-permute-start | bytes 233480 | tf_op jit(solution)/shard_map/ppermute | solution.py:41
  104.3 5.2 %collective-permute-start.19 = (f32[19,8,1,128]{3,2,1,0:T(1,128)S(1)}, f32[19,8,1,128]{3,2,1,0:T(1,128)S(1)}, u32[]{:S(2)}, u32[]{:S(2)}) collective-permute-start(f32[19,8,1,128]{3,2,1,0:T(1,128)S(1)} %get-tuple-element.145), channel_id=1, source_target_pairs={{8,0},{16,8},{24,16},{0,24},{9,1},{17,9},{25,17},{1,25},{10,2},{18... | collective-permute-start | bytes 233480 | tf_op jit(solution)/shard_map/ppermute | solution.py:42
  111.5 3.7 %collective-permute-start.20 = (f32[19,8,10,1]{0,1,3,2:T(8,128)}, f32[19,8,10,1]{0,1,3,2:T(8,128)S(1)}, u32[]{:S(2)}, u32[]{:S(2)}) collective-permute-start(f32[19,8,10,1]{0,1,3,2:T(8,128)} %copy.218), channel_id=1, source_target_pairs={{0,2},{2,4},{4,6},{6,0},{1,3},{3,5},{5,7},{7,1},{8,10},{10,12},{12... | collective-permute-start | bytes 18248 | tf_op jit(solution)/shard_map/ppermute | solution.py:41
  112.2 4.4 %collective-permute-start.21 = (f32[19,8,10,1]{0,1,3,2:T(8,128)S(1)}, f32[19,8,10,1]{0,1,3,2:T(8,128)}, u32[]{:S(2)}, u32[]{:S(2)}) collective-permute-start(f32[19,8,10,1]{0,1,3,2:T(8,128)S(1)} %copy.220), channel_id=1, source_target_pairs={{2,0},{4,2},{6,4},{0,6},{3,1},{5,3},{7,5},{1,7},{10,8},{12,10},{14... | collective-permute-start | bytes 18248 | tf_op jit(solution)/shard_map/ppermute | solution.py:42
  119.3 10.3 %collective-permute-start.22 = (f32[19,1,10,130]{3,2,1,0:T(8,128)S(1)}, f32[19,1,10,130]{3,2,1,0:T(8,128)S(1)}, u32[]{:S(2)}, u32[]{:S(2)}) collective-permute-start(f32[19,1,10,130]{3,2,1,0:T(8,128)S(1)} %get-tuple-element.129), channel_id=1, source_target_pairs={{0,1},{1,0},{2,3},{3,2},{4,5},{5,4},{6,7},{7,6},{8,9},{9,8},{10,11... | collective-permute-start | bytes 296408 | tf_op jit(solution)/shard_map/ppermute | solution.py:41
  119.9 14.3 %collective-permute-start.23 = (f32[19,1,10,130]{3,2,1,0:T(8,128)S(1)}, f32[19,1,10,130]{3,2,1,0:T(8,128)S(1)}, u32[]{:S(2)}, u32[]{:S(2)}) collective-permute-start(f32[19,1,10,130]{3,2,1,0:T(8,128)S(1)} %get-tuple-element.130), channel_id=1, source_target_pairs={{1,0},{0,1},{3,2},{2,3},{5,4},{4,5},{7,6},{6,7},{9,8},{8,9},{11,10... | collective-permute-start | bytes 296408 | tf_op jit(solution)/shard_map/ppermute | solution.py:42
  (56 other events, 313.5 us)
where the time goes:
time: 193 us; the launch traced here: 192 us
  waiting for transfers between devices  78.8 us (41%)
  blocking collectives  44.2 us (23%)
  local copies, waits for them, and re-layouts  23.9 us (12%)
  starting transfers between devices  21.7 us (11%)
  other arithmetic  13.1 us (7%)
  between operations  9.94 us (5%)
    psum x1, blocking collectives, per_device(): lax.psum((local_terms[0], local_terms[1], local_terms[2], local_terms[3],...  44.2 us
    ppermute x12, waiting for transfers between devices, extended(): before = lax.ppermute(last, axis, up)  39.9 us
    ppermute x12, waiting for transfers between devices, extended(): after = lax.ppermute(first, axis, down)  38.8 us
    ppermute x12, starting transfers between devices, extended(): after = lax.ppermute(first, axis, down)  12.2 us
    ppermute x12, starting transfers between devices, extended(): before = lax.ppermute(last, axis, up)  9.54 us
    ppermute x4, local copies, waits for them, and re-layouts, extended(): after = lax.ppermute(first, axis, down)  6.25 us
    unnamed x90, other arithmetic  5.58 us
    ppermute x4, local copies, waits for them, and re-layouts, extended(): before = lax.ppermute(last, axis, up)  5.46 us
  transfers between devices with their start and end apart: 24, of which 23 were waited for; matrix products, arithmetic and copies ran while one was open for 4% of the time, Pallas kernels for 0%

commit v1 on v0

--- a/solution.py
+++ b/solution.py
@@ -140,19 +140,22 @@
         energy_base,
         energy_cross,
     ) = lax.psum(
-        (
-            local_terms[0],
-            local_terms[1],
-            local_terms[2],
-            local_terms[3],
-            local_terms[4],
-            local_terms[5],
-            local_terms[6],
-            local_terms[7],
-            local_terms[8],
-            local_terms[9],
+        lax.psum(
+            (
+                local_terms[0],
+                local_terms[1],
+                local_terms[2],
+                local_terms[3],
+                local_terms[4],
+                local_terms[5],
+                local_terms[6],
+                local_terms[7],
+                local_terms[8],
+                local_terms[9],
+            ),
+            ("gy", "gz"),
         ),
-        ("gx", "gy", "gz"),
+        "gx",
     )
     change = (change_rho + change_mom) / cells
     gain = JUMP / (1.0 + limiter * change)

time: 193 us -> 180 us (0.933)
  the two profiles are of different devices: /device:TPU:12 before, /device:TPU:0 now
where the time goes in v1:
time: 180 us; the launch traced here: 179 us
  waiting for transfers between devices  79.2 us (44%)
  blocking collectives  27.8 us (15%)
  starting transfers between devices  25.2 us (14%)
  local copies, waits for them, and re-layouts  23.9 us (13%)
  other arithmetic  13.1 us (7%)
  between operations  9.92 us (6%)
    ppermute x12, waiting for transfers between devices, extended(): before = lax.ppermute(last, axis, up)  41.7 us
    ppermute x12, waiting for transfers between devices, extended(): after = lax.ppermute(first, axis, down)  37.6 us
    ppermute x12, starting transfers between devices, extended(): after = lax.ppermute(first, axis, down)  16.9 us
    psum x1, blocking collectives, per_device(): lax.psum((local_terms[0], local_terms[1], local_terms[2], local_terms[3],...  14.7 us
    psum x1, blocking collectives, per_device(): lax.psum(lax.psum((local_terms[0], local_terms[1], local_terms[2], local_...  13.1 us
    ppermute x12, starting transfers between devices, extended(): before = lax.ppermute(last, axis, up)  8.35 us
    ppermute x4, local copies, waits for them, and re-layouts, extended(): after = lax.ppermute(first, axis, down)  6.25 us
    unnamed x90, other arithmetic  5.58 us
  transfers between devices with their start and end apart: 24, of which 22 were waited for; matrix products, arithmetic and copies ran while one was open for 5% of the time, Pallas kernels for 0%

profile of v1, /device:TPU:0, one launch (start us, length us, event | category | flops | bytes accessed | tf_op | source)
XLA Modules:
  0.0 179.2 jit_solution(12202767819091923919)
XLA Ops:
  5.4 5.1 %collective-permute-start = (f32[19,8,1,128]{3,2,1,0:T(1,128)S(1)}, f32[19,8,1,128]{3,2,1,0:T(1,128)S(1)}, u32[]{:S(2)}, u32[]{:S(2)}) collective-permute-start(f32[19,8,1,128]{3,2,1,0:T(1,128)S(1)} %get-tuple-element.162), channel_id=1, source_target_pairs={{8,0},{16,8},{24,16},{0,24},{9,1},{17,9},{25,17},{1,25},{10,2},{18... | collective-permute-start | bytes 233480 | tf_op jit(solution)/shard_map/ppermute | solution.py:42
  10.5 2.4 %collective-permute-done = f32[19,8,1,128]{3,2,1,0:T(1,128)S(1)} collective-permute-done((f32[19,8,1,128]{3,2,1,0:T(1,128)S(1)}, f32[19,8,1,128]{3,2,1,0:T(1,128)S(1)}, u32[]{:S(2)}, u32[]{:S(2)}) %collective-permute-start) | collective-permute-done | bytes 77856 | tf_op jit(solution)/shard_map/ppermute | solution.py:42
  13.0 3.7 %collective-permute-done.1 = f32[19,8,1,128]{3,2,1,0:T(1,128)S(1)} collective-permute-done((f32[19,8,1,128]{3,2,1,0:T(1,128)S(1)}, f32[19,8,1,128]{3,2,1,0:T(1,128)S(1)}, u32[]{:S(2)}, u32[]{:S(2)}) %collective-permute-start.1) | collective-permute-done | bytes 77856 | tf_op jit(solution)/shard_map/ppermute | solution.py:41
  24.1 1.6 collective-permute-start.4
  26.3 8.1 %collective-permute-done.4 = f32[19,1,10,130]{3,2,1,0:T(8,128)S(1)} collective-permute-done((f32[19,1,10,130]{3,2,1,0:T(8,128)S(1)}, f32[19,1,10,130]{3,2,1,0:T(8,128)S(1)}, u32[]{:S(2)}, u32[]{:S(2)}) %collective-permute-start.4) | collective-permute-done | bytes 98832 | tf_op jit(solution)/shard_map/ppermute | solution.py:42
  34.4 6.2 %collective-permute-done.5 = f32[19,1,10,130]{3,2,1,0:T(8,128)S(1)} collective-permute-done((f32[19,1,10,130]{3,2,1,0:T(8,128)S(1)}, f32[19,1,10,130]{3,2,1,0:T(8,128)S(1)}, u32[]{:S(2)}, u32[]{:S(2)}) %collective-permute-start.5) | collective-permute-done | bytes 98832 | tf_op jit(solution)/shard_map/ppermute | solution.py:41
  44.3 2.4 %collective-permute-done.6 = f32[19,8,1,128]{3,2,1,0:T(1,128)S(1)} collective-permute-done((f32[19,8,1,128]{3,2,1,0:T(1,128)S(1)}, f32[19,8,1,128]{3,2,1,0:T(1,128)S(1)}, u32[]{:S(2)}, u32[]{:S(2)}) %collective-permute-start.6) | collective-permute-done | bytes 77856 | tf_op jit(solution)/shard_map/ppermute | solution.py:42
  46.7 2.3 %collective-permute-done.7 = f32[19,8,1,128]{3,2,1,0:T(1,128)S(1)} collective-permute-done((f32[19,8,1,128]{3,2,1,0:T(1,128)S(1)}, f32[19,8,1,128]{3,2,1,0:T(1,128)S(1)}, u32[]{:S(2)}, u32[]{:S(2)}) %collective-permute-start.7) | collective-permute-done | bytes 77856 | tf_op jit(solution)/shard_map/ppermute | solution.py:41
  58.8 8.1 %collective-permute-done.10 = f32[19,1,10,130]{3,2,1,0:T(8,128)S(1)} collective-permute-done((f32[19,1,10,130]{3,2,1,0:T(8,128)S(1)}, f32[19,1,10,130]{3,2,1,0:T(8,128)S(1)}, u32[]{:S(2)}, u32[]{:S(2)}) %collective-permute-start.10) | collective-permute-done | bytes 98832 | tf_op jit(solution)/shard_map/ppermute | solution.py:42
  66.9 5.1 %collective-permute-done.11 = f32[19,1,10,130]{3,2,1,0:T(8,128)S(1)} collective-permute-done((f32[19,1,10,130]{3,2,1,0:T(8,128)S(1)}, f32[19,1,10,130]{3,2,1,0:T(8,128)S(1)}, u32[]{:S(2)}, u32[]{:S(2)}) %collective-permute-start.11) | collective-permute-done | bytes 98832 | tf_op jit(solution)/shard_map/ppermute | solution.py:41
  73.8 1.9 %collective-permute-start.13 = (f32[19,8,1,128]{3,2,1,0:T(1,128)S(1)}, f32[19,8,1,128]{3,2,1,0:T(1,128)S(1)}, u32[]{:S(2)}, u32[]{:S(2)}) collective-permute-start(f32[19,8,1,128]{3,2,1,0:T(1,128)S(1)} %get-tuple-element.157), channel_id=1, source_target_pairs={{0,8},{8,16},{16,24},{24,0},{1,9},{9,17},{17,25},{25,1},{2,10},{10... | collective-permute-start | bytes 233480 | tf_op jit(solution)/shard_map/ppermute | solution.py:41
  75.7 2.7 %collective-permute-done.12 = f32[19,8,1,128]{3,2,1,0:T(1,128)S(1)} collective-permute-done((f32[19,8,1,128]{3,2,1,0:T(1,128)S(1)}, f32[19,8,1,128]{3,2,1,0:T(1,128)S(1)}, u32[]{:S(2)}, u32[]{:S(2)}) %collective-permute-start.12) | collective-permute-done | bytes 77856 | tf_op jit(solution)/shard_map/ppermute | solution.py:42
  84.4 1.6 collective-permute-done.15
  90.1 8.1 %collective-permute-done.16 = f32[19,1,10,130]{3,2,1,0:T(8,128)S(1)} collective-permute-done((f32[19,1,10,130]{3,2,1,0:T(8,128)S(1)}, f32[19,1,10,130]{3,2,1,0:T(8,128)S(1)}, u32[]{:S(2)}, u32[]{:S(2)}) %collective-permute-start.16) | collective-permute-done | bytes 98832 | tf_op jit(solution)/shard_map/ppermute | solution.py:42
  98.2 6.4 %collective-permute-done.17 = f32[19,1,10,130]{3,2,1,0:T(8,128)S(1)} collective-permute-done((f32[19,1,10,130]{3,2,1,0:T(8,128)S(1)}, f32[19,1,10,130]{3,2,1,0:T(8,128)S(1)}, u32[]{:S(2)}, u32[]{:S(2)}) %collective-permute-start.17) | collective-permute-done | bytes 98832 | tf_op jit(solution)/shard_map/ppermute | solution.py:41
  106.9 3.8 %collective-permute-start.19 = (f32[19,8,1,128]{3,2,1,0:T(1,128)S(1)}, f32[19,8,1,128]{3,2,1,0:T(1,128)S(1)}, u32[]{:S(2)}, u32[]{:S(2)}) collective-permute-start(f32[19,8,1,128]{3,2,1,0:T(1,128)S(1)} %get-tuple-element.155), channel_id=1, source_target_pairs={{8,0},{16,8},{24,16},{0,24},{9,1},{17,9},{25,17},{1,25},{10,2},{18... | collective-permute-start | bytes 233480 | tf_op jit(solution)/shard_map/ppermute | solution.py:42
  110.7 2.9 %collective-permute-done.18 = f32[19,8,1,128]{3,2,1,0:T(1,128)S(1)} collective-permute-done((f32[19,8,1,128]{3,2,1,0:T(1,128)S(1)}, f32[19,8,1,128]{3,2,1,0:T(1,128)S(1)}, u32[]{:S(2)}, u32[]{:S(2)}) %collective-permute-start.18) | collective-permute-done | bytes 77856 | tf_op jit(solution)/shard_map/ppermute | solution.py:41
  116.3 1.8 collective-permute-start.21
  120.8 2.2 %copy.221 = f32[19,8,10,1]{3,2,1,0:T(8,128)S(1)} copy(f32[19,8,10,1]{0,1,3,2:T(8,128)} %collective-permute-done.21) | data formatting | bytes 12160 | tf_op jit(solution)/shard_map/ppermute | solution.py:42
  123.5 1.6 collective-permute-start.22
  125.7 8.1 %collective-permute-done.22 = f32[19,1,10,130]{3,2,1,0:T(8,128)S(1)} collective-permute-done((f32[19,1,10,130]{3,2,1,0:T(8,128)S(1)}, f32[19,1,10,130]{3,2,1,0:T(8,128)S(1)}, u32[]{:S(2)}, u32[]{:S(2)}) %collective-permute-start.22) | collective-permute-done | bytes 98832 | tf_op jit(solution)/shard_map/ppermute | solution.py:41
  133.8 4.5 %collective-permute-done.23 = f32[19,1,10,130]{3,2,1,0:T(8,128)S(1)} collective-permute-done((f32[19,1,10,130]{3,2,1,0:T(8,128)S(1)}, f32[19,1,10,130]{3,2,1,0:T(8,128)S(1)}, u32[]{:S(2)}, u32[]{:S(2)}) %collective-permute-start.23) | collective-permute-done | bytes 98832 | tf_op jit(solution)/shard_map/ppermute | solution.py:42
  141.9 14.7 %all-reduce = (f32[]{:T(128)}, f32[]{:T(128)}, f32[]{:T(128)}, f32[]{:T(128)}, f32[]{:T(128)}, /*index=5*/f32[]{:T(128)}, f32[]{:T(128)}, f32[]{:T(128)}, f32[]{:T(128)}, f32[]{:T(128)}) all-reduce(f32[]{:T(128)} %fusion.287, f32[]{:T(128)} %get-tuple-element.5, ...), channel_id=1, replica_groups=mesh['gx'=4,'gy'=4,'gz'=2] {'gy','gz'}, use_global_device_ids=true, to_apply=%region_2.3 | all-reduce | flops 10 | bytes 80 | tf_op jit(solution)/shard_map/psum | solution.py:143
  156.7 13.1 %all-reduce.1 = (f32[]{:T(128)}, f32[]{:T(128)}, f32[]{:T(128)}, f32[]{:T(128)}, f32[]{:T(128)}, /*index=5*/f32[]{:T(128)}, f32[]{:T(128)}, f32[]{:T(128)}, f32[]{:T(128)}, f32[]{:T(128)}) all-reduce(f32[]{:T(128)} %get-tuple-element.13, f32[]{:T(128)} %get-tuple-element.14, ...), channel_id=1, replica_groups=mesh['gx'=4,'gy'=4,'gz'=2] {'gx'}, use_global_device_ids=true, to_apply=%region_3.4 | all-reduce | flops 10 | bytes 80 | tf_op jit(solution)/shard_map/psum | solution.py:142
  (382 shorter events, 50.8 us)
Async XLA Ops:
  5.4 7.6 %collective-permute-start = (f32[19,8,1,128]{3,2,1,0:T(1,128)S(1)}, f32[19,8,1,128]{3,2,1,0:T(1,128)S(1)}, u32[]{:S(2)}, u32[]{:S(2)}) collective-permute-start(f32[19,8,1,128]{3,2,1,0:T(1,128)S(1)} %get-tuple-element.162), channel_id=1, source_target_pairs={{8,0},{16,8},{24,16},{0,24},{9,1},{17,9},{25,17},{1,25},{10,2},{18... | collective-permute-start | bytes 233480 | tf_op jit(solution)/shard_map/ppermute | solution.py:42
  10.5 6.2 %collective-permute-start.1 = (f32[19,8,1,128]{3,2,1,0:T(1,128)S(1)}, f32[19,8,1,128]{3,2,1,0:T(1,128)S(1)}, u32[]{:S(2)}, u32[]{:S(2)}) collective-permute-start(f32[19,8,1,128]{3,2,1,0:T(1,128)S(1)} %get-tuple-element.161), channel_id=1, source_target_pairs={{0,8},{8,16},{16,24},{24,0},{1,9},{9,17},{17,25},{25,1},{2,10},{10... | collective-permute-start | bytes 233480 | tf_op jit(solution)/shard_map/ppermute | solution.py:41
  18.1 1.7 collective-permute-start.2
  18.8 3.5 %collective-permute-start.3 = (f32[19,8,10,1]{0,1,3,2:T(8,128)S(1)}, f32[19,8,10,1]{0,1,3,2:T(8,128)S(1)}, u32[]{:S(2)}, u32[]{:S(2)}) collective-permute-start(f32[19,8,10,1]{0,1,3,2:T(8,128)S(1)} %copy.202), channel_id=1, source_target_pairs={{0,2},{2,4},{4,6},{6,0},{1,3},{3,5},{5,7},{7,1},{8,10},{10,12},{12... | collective-permute-start | bytes 18248 | tf_op jit(solution)/shard_map/ppermute | solution.py:41
  24.1 10.3 %collective-permute-start.4 = (f32[19,1,10,130]{3,2,1,0:T(8,128)S(1)}, f32[19,1,10,130]{3,2,1,0:T(8,128)S(1)}, u32[]{:S(2)}, u32[]{:S(2)}) collective-permute-start(f32[19,1,10,130]{3,2,1,0:T(8,128)S(1)} %get-tuple-element.146), channel_id=1, source_target_pairs={{1,0},{0,1},{3,2},{2,3},{5,4},{4,5},{7,6},{6,7},{9,8},{8,9},{11,10... | collective-permute-start | bytes 296408 | tf_op jit(solution)/shard_map/ppermute | solution.py:42
  25.7 14.9 %collective-permute-start.5 = (f32[19,1,10,130]{3,2,1,0:T(8,128)S(1)}, f32[19,1,10,130]{3,2,1,0:T(8,128)S(1)}, u32[]{:S(2)}, u32[]{:S(2)}) collective-permute-start(f32[19,1,10,130]{3,2,1,0:T(8,128)S(1)} %get-tuple-element.145), channel_id=1, source_target_pairs={{0,1},{1,0},{2,3},{3,2},{4,5},{5,4},{6,7},{7,6},{8,9},{9,8},{10,11... | collective-permute-start | bytes 296408 | tf_op jit(solution)/shard_map/ppermute | solution.py:41
  42.2 4.5 %collective-permute-start.6 = (f32[19,8,1,128]{3,2,1,0:T(1,128)S(1)}, f32[19,8,1,128]{3,2,1,0:T(1,128)S(1)}, u32[]{:S(2)}, u32[]{:S(2)}) collective-permute-start(f32[19,8,1,128]{3,2,1,0:T(1,128)S(1)} %get-tuple-element.160), channel_id=1, source_target_pairs={{8,0},{16,8},{24,16},{0,24},{9,1},{17,9},{25,17},{1,25},{10,2},{18... | collective-permute-start | bytes 233480 | tf_op jit(solution)/shard_map/ppermute | solution.py:42
  42.8 6.2 %collective-permute-start.7 = (f32[19,8,1,128]{3,2,1,0:T(1,128)S(1)}, f32[19,8,1,128]{3,2,1,0:T(1,128)S(1)}, u32[]{:S(2)}, u32[]{:S(2)}) collective-permute-start(f32[19,8,1,128]{3,2,1,0:T(1,128)S(1)} %get-tuple-element.159), channel_id=1, source_target_pairs={{0,8},{8,16},{16,24},{24,0},{1,9},{9,17},{17,25},{25,1},{2,10},{10... | collective-permute-start | bytes 233480 | tf_op jit(solution)/shard_map/ppermute | solution.py:41
  50.4 1.7 collective-permute-start.8
  51.1 3.6 %collective-permute-start.9 = (f32[19,8,10,1]{0,1,3,2:T(8,128)S(1)}, f32[19,8,10,1]{0,1,3,2:T(8,128)S(1)}, u32[]{:S(2)}, u32[]{:S(2)}) collective-permute-start(f32[19,8,10,1]{0,1,3,2:T(8,128)S(1)} %copy.208), channel_id=1, source_target_pairs={{0,2},{2,4},{4,6},{6,0},{1,3},{3,5},{5,7},{7,1},{8,10},{10,12},{12... | collective-permute-start | bytes 18248 | tf_op jit(solution)/shard_map/ppermute | solution.py:41
  56.6 10.3 %collective-permute-start.10 = (f32[19,1,10,130]{3,2,1,0:T(8,128)S(1)}, f32[19,1,10,130]{3,2,1,0:T(8,128)S(1)}, u32[]{:S(2)}, u32[]{:S(2)}) collective-permute-start(f32[19,1,10,130]{3,2,1,0:T(8,128)S(1)} %get-tuple-element.144), channel_id=1, source_target_pairs={{1,0},{0,1},{3,2},{2,3},{5,4},{4,5},{7,6},{6,7},{9,8},{8,9},{11,10... | collective-permute-start | bytes 296408 | tf_op jit(solution)/shard_map/ppermute | solution.py:42
  58.2 13.8 %collective-permute-start.11 = (f32[19,1,10,130]{3,2,1,0:T(8,128)S(1)}, f32[19,1,10,130]{3,2,1,0:T(8,128)S(1)}, u32[]{:S(2)}, u32[]{:S(2)}) collective-permute-start(f32[19,1,10,130]{3,2,1,0:T(8,128)S(1)} %get-tuple-element.143), channel_id=1, source_target_pairs={{0,1},{1,0},{2,3},{3,2},{4,5},{5,4},{6,7},{7,6},{8,9},{9,8},{10,11... | collective-permute-start | bytes 296408 | tf_op jit(solution)/shard_map/ppermute | solution.py:41
  73.6 4.8 %collective-permute-start.12 = (f32[19,8,1,128]{3,2,1,0:T(1,128)S(1)}, f32[19,8,1,128]{3,2,1,0:T(1,128)S(1)}, u32[]{:S(2)}, u32[]{:S(2)}) collective-permute-start(f32[19,8,1,128]{3,2,1,0:T(1,128)S(1)} %get-tuple-element.158), channel_id=1, source_target_pairs={{8,0},{16,8},{24,16},{0,24},{9,1},{17,9},{25,17},{1,25},{10,2},{18... | collective-permute-start | bytes 233480 | tf_op jit(solution)/shard_map/ppermute | solution.py:42
  73.8 6.2 %collective-permute-start.13 = (f32[19,8,1,128]{3,2,1,0:T(1,128)S(1)}, f32[19,8,1,128]{3,2,1,0:T(1,128)S(1)}, u32[]{:S(2)}, u32[]{:S(2)}) collective-permute-start(f32[19,8,1,128]{3,2,1,0:T(1,128)S(1)} %get-tuple-element.157), channel_id=1, source_target_pairs={{0,8},{8,16},{16,24},{24,0},{1,9},{9,17},{17,25},{25,1},{2,10},{10... | collective-permute-start | bytes 233480 | tf_op jit(solution)/shard_map/ppermute | solution.py:41
  81.3 1.7 collective-permute-start.14
  82.1 3.9 %collective-permute-start.15 = (f32[19,8,10,1]{0,1,3,2:T(8,128)S(1)}, f32[19,8,10,1]{0,1,3,2:T(8,128)S(1)}, u32[]{:S(2)}, u32[]{:S(2)}) collective-permute-start(f32[19,8,10,1]{0,1,3,2:T(8,128)S(1)} %copy.214), channel_id=1, source_target_pairs={{0,2},{2,4},{4,6},{6,0},{1,3},{3,5},{5,7},{7,1},{8,10},{10,12},{12... | collective-permute-start | bytes 18248 | tf_op jit(solution)/shard_map/ppermute | solution.py:41
  87.9 10.3 %collective-permute-start.16 = (f32[19,1,10,130]{3,2,1,0:T(8,128)S(1)}, f32[19,1,10,130]{3,2,1,0:T(8,128)S(1)}, u32[]{:S(2)}, u32[]{:S(2)}) collective-permute-start(f32[19,1,10,130]{3,2,1,0:T(8,128)S(1)} %get-tuple-element.142), channel_id=1, source_target_pairs={{1,0},{0,1},{3,2},{2,3},{5,4},{4,5},{7,6},{6,7},{9,8},{8,9},{11,10... | collective-permute-start | bytes 296408 | tf_op jit(solution)/shard_map/ppermute | solution.py:42
  89.5 15.1 %collective-permute-start.17 = (f32[19,1,10,130]{3,2,1,0:T(8,128)S(1)}, f32[19,1,10,130]{3,2,1,0:T(8,128)S(1)}, u32[]{:S(2)}, u32[]{:S(2)}) collective-permute-start(f32[19,1,10,130]{3,2,1,0:T(8,128)S(1)} %get-tuple-element.141), channel_id=1, source_target_pairs={{0,1},{1,0},{2,3},{3,2},{4,5},{5,4},{6,7},{7,6},{8,9},{9,8},{10,11... | collective-permute-start | bytes 296408 | tf_op jit(solution)/shard_map/ppermute | solution.py:41
  106.8 6.7 %collective-permute-start.18 = (f32[19,8,1,128]{3,2,1,0:T(1,128)S(1)}, f32[19,8,1,128]{3,2,1,0:T(1,128)S(1)}, u32[]{:S(2)}, u32[]{:S(2)}) collective-permute-start(f32[19,8,1,128]{3,2,1,0:T(1,128)S(1)} %get-tuple-element.156), channel_id=1, source_target_pairs={{0,8},{8,16},{16,24},{24,0},{1,9},{9,17},{17,25},{25,1},{2,10},{10... | collective-permute-start | bytes 233480 | tf_op jit(solution)/shard_map/ppermute | solution.py:41
  106.9 6.7 %collective-permute-start.19 = (f32[19,8,1,128]{3,2,1,0:T(1,128)S(1)}, f32[19,8,1,128]{3,2,1,0:T(1,128)S(1)}, u32[]{:S(2)}, u32[]{:S(2)}) collective-permute-start(f32[19,8,1,128]{3,2,1,0:T(1,128)S(1)} %get-tuple-element.155), channel_id=1, source_target_pairs={{8,0},{16,8},{24,16},{0,24},{9,1},{17,9},{25,17},{1,25},{10,2},{18... | collective-permute-start | bytes 233480 | tf_op jit(solution)/shard_map/ppermute | solution.py:42
  115.6 3.9 %collective-permute-start.20 = (f32[19,8,10,1]{0,1,3,2:T(8,128)}, f32[19,8,10,1]{0,1,3,2:T(8,128)S(1)}, u32[]{:S(2)}, u32[]{:S(2)}) collective-permute-start(f32[19,8,10,1]{0,1,3,2:T(8,128)} %copy.218), channel_id=1, source_target_pairs={{0,2},{2,4},{4,6},{6,0},{1,3},{3,5},{5,7},{7,1},{8,10},{10,12},{12... | collective-permute-start | bytes 18248 | tf_op jit(solution)/shard_map/ppermute | solution.py:41
  116.3 4.5 %collective-permute-start.21 = (f32[19,8,10,1]{0,1,3,2:T(8,128)S(1)}, f32[19,8,10,1]{0,1,3,2:T(8,128)}, u32[]{:S(2)}, u32[]{:S(2)}) collective-permute-start(f32[19,8,10,1]{0,1,3,2:T(8,128)S(1)} %copy.220), channel_id=1, source_target_pairs={{2,0},{4,2},{6,4},{0,6},{3,1},{5,3},{7,5},{1,7},{10,8},{12,10},{14... | collective-permute-start | bytes 18248 | tf_op jit(solution)/shard_map/ppermute | solution.py:42
  123.5 10.3 %collective-permute-start.22 = (f32[19,1,10,130]{3,2,1,0:T(8,128)S(1)}, f32[19,1,10,130]{3,2,1,0:T(8,128)S(1)}, u32[]{:S(2)}, u32[]{:S(2)}) collective-permute-start(f32[19,1,10,130]{3,2,1,0:T(8,128)S(1)} %get-tuple-element.139), channel_id=1, source_target_pairs={{0,1},{1,0},{2,3},{3,2},{4,5},{5,4},{6,7},{7,6},{8,9},{9,8},{10,11... | collective-permute-start | bytes 296408 | tf_op jit(solution)/shard_map/ppermute | solution.py:41
  125.1 13.1 %collective-permute-start.23 = (f32[19,1,10,130]{3,2,1,0:T(8,128)S(1)}, f32[19,1,10,130]{3,2,1,0:T(8,128)S(1)}, u32[]{:S(2)}, u32[]{:S(2)}) collective-permute-start(f32[19,1,10,130]{3,2,1,0:T(8,128)S(1)} %get-tuple-element.140), channel_id=1, source_target_pairs={{1,0},{0,1},{3,2},{2,3},{5,4},{4,5},{7,6},{6,7},{9,8},{8,9},{11,10... | collective-permute-start | bytes 296408 | tf_op jit(solution)/shard_map/ppermute | solution.py:42
  (56 other events, 307.1 us)
